TPU v7x, 256 devices: a whole 4x4x8 slice. The times are simulated.
256 devices in a mesh: row: 32 (over y, z), col: 8 (over x, core).
Axes of the slice: x: 4, y: 4, z: 8, core: 2. Of those that a mesh axis runs over, the one named last changes fastest.
Arguments:
- sim_window: bfloat16 [6144, 6144], P('row', 'col'), as said below
- sim_rest: bfloat16 [6144, 113856], P('row', 'col'), may hold values from -6 to 6
- joined_partner_pairs: int32 [768, 2], replicated, may hold values from 0 to 6143, as said below
- cluster_member_count: int32 [6144], replicated, may hold values from 1 to 64
Outputs:
- window_out: bfloat16 [6144, 6144], P('row', 'col')
- rest_out: bfloat16 [6144, 113856], P('row', 'col')
Inputs may be any that keep to these rules, and one draw needn't show every extreme that they name: `joined_partner_pairs`: each row is (survivor, partner); no window item appears twice in the whole list. Each aligned block of 192 items holds exactly 24 partners. For any two aligned blocks (possibly the same), at most 3 pairs have their partner in the first and their survivor in the second, and some two blocks have exactly 3. Nearly symmetric: sim_window[i, j] is close to sim_window[j, i].
All inputs are finite; a program needn't handle non-finite values.
Results may differ from a plain program's by a relative error of at most 0.001.
Values may be sent and summed in bfloat16 or wider, within the bound.
No kernel may reach another device: no remote copies, remote signals or barrier semaphores. Data moves between devices by JAX's collectives and lax.ppermute only.
A program may use at most 128 MiB of HBM per device.

v0:
```python
import jax
import jax.numpy as jnp
from jax import lax
from jax.sharding import PartitionSpec as P


def pairing_tables(joined_partner_pairs, cluster_member_count):
    lasting_node = joined_partner_pairs[:, 0]
    vanishing_node = joined_partner_pairs[:, 1]
    remaining_size = cluster_member_count[lasting_node].astype(jnp.float32)
    absorbed_size = cluster_member_count[vanishing_node].astype(jnp.float32)
    joined_cluster_size = remaining_size + absorbed_size
    return (
        lasting_node,
        vanishing_node,
        remaining_size / joined_cluster_size,
        absorbed_size / joined_cluster_size,
    )


def item_weight_values(node_labels, lasting_node, vanishing_node, retained_pair, selected_pair):
    lasting_mask = node_labels[:, None] == lasting_node[None, :]
    belongs_mask = node_labels[:, None] == vanishing_node[None, :]
    lasting_real_mask = lasting_mask.astype(jnp.float32)
    matched_mask = jnp.sum((lasting_mask | belongs_mask).astype(jnp.float32), axis=1)
    retained_entries = (
        1.0 - matched_mask + jnp.sum(lasting_real_mask * retained_pair[None, :], axis=1)
    )
    selected_entries = jnp.sum(lasting_real_mask * selected_pair[None, :], axis=1)
    donor_position = jnp.sum(jnp.where(lasting_mask, vanishing_node[None, :], 0), axis=1)
    return (retained_entries, selected_entries, donor_position)


def shards(sim_window, sim_rest, joined_partner_pairs, cluster_member_count):
    row_number_total = sim_window.shape[0]
    col_count = sim_window.shape[1]
    blocks = lax.axis_size("row")
    local_block = lax.axis_index("row")
    my_col = lax.axis_index("col")
    lasting_node, vanishing_node, retained_pair, selected_pair = pairing_tables(
        joined_partner_pairs, cluster_member_count
    )
    row_sequence = jnp.arange(row_number_total, dtype=jnp.int32)
    retained_entries, selected_entries, ignored = item_weight_values(
        local_block * row_number_total + row_sequence,
        lasting_node,
        vanishing_node,
        retained_pair,
        selected_pair,
    )
    src_block = vanishing_node // row_number_total
    destination_block = lasting_node // row_number_total
    pair_count = joined_partner_pairs.shape[0]
    pair_order = jnp.arange(pair_count, dtype=jnp.int32)
    earlier = pair_order[None, :] < pair_order[:, None]
    slot_width = row_number_total // 8
    same_route = src_block[None, :] == src_block[:, None]
    slot_rank = jnp.sum((earlier & same_route).astype(jnp.int32), axis=1)
    recv_slot = src_block * slot_width + slot_rank
    recv_width = blocks * slot_width
    mine_src = src_block == local_block
    slot_hot = (
        (jnp.arange(slot_width, dtype=jnp.int32)[:, None] == slot_rank[None, :]) & mine_src[None, :]
    ).astype(jnp.bfloat16)
    row_hot = (
        (vanishing_node - local_block * row_number_total)[:, None] == row_sequence[None, :]
    ).astype(jnp.bfloat16)
    selector = jnp.dot(slot_hot, row_hot, preferred_element_type=jnp.float32).astype(jnp.bfloat16)
    send_window = jnp.dot(selector, sim_window, preferred_element_type=jnp.float32).astype(
        jnp.bfloat16
    )
    send_rest = jnp.dot(selector, sim_rest, preferred_element_type=jnp.float32).astype(jnp.bfloat16)
    local_destination = destination_block == local_block
    target_hot = (
        ((lasting_node - local_block * row_number_total)[None, :] == row_sequence[:, None])
        & local_destination[None, :]
    ).astype(jnp.bfloat16)
    recv_hot = (recv_slot[:, None] == jnp.arange(recv_width, dtype=jnp.int32)[None, :]).astype(
        jnp.bfloat16
    )
    placement = jnp.dot(target_hot, recv_hot, preferred_element_type=jnp.float32).astype(
        jnp.bfloat16
    )
    placed_window = jnp.dot(
        placement,
        lax.all_gather(send_window, "row", axis=0, tiled=True),
        preferred_element_type=jnp.float32,
    )
    placed_rest = jnp.dot(
        placement,
        lax.all_gather(send_rest, "row", axis=0, tiled=True),
        preferred_element_type=jnp.float32,
    )
    mixed_window = (
        retained_entries[:, None] * sim_window.astype(jnp.float32)
        + selected_entries[:, None] * placed_window
    ).astype(jnp.bfloat16)
    rest_out = (
        retained_entries[:, None] * sim_rest.astype(jnp.float32)
        + selected_entries[:, None] * placed_rest
    ).astype(jnp.bfloat16)
    col_iota = jnp.arange(col_count, dtype=jnp.int32)
    column_identifiers = my_col * col_count + col_iota
    column_retained, column_selected, column_provider = item_weight_values(
        column_identifiers, lasting_node, vanishing_node, retained_pair, selected_pair
    )
    piece = lax.all_gather(mixed_window, "col", axis=1, tiled=True)
    piece_width = piece.shape[1]
    picker = (jnp.arange(piece_width, dtype=jnp.int32)[:, None] == column_provider[None, :]).astype(
        jnp.bfloat16
    )
    gathered = jnp.dot(piece, picker, preferred_element_type=jnp.float32)
    window_out = (
        column_retained[None, :] * mixed_window.astype(jnp.float32)
        + column_selected[None, :] * gathered
    ).astype(jnp.bfloat16)
    return (window_out, rest_out)


def solution(mesh):
    in_specs = (P("row", "col"), P("row", "col"), P(), P())
    out_specs = (P("row", "col"), P("row", "col"))
    return jax.shard_map(shards, mesh=mesh, in_specs=in_specs, out_specs=out_specs, check_vma=False)
```

profile of v0, /device:TPU:1, one launch (start us, length us, event | category | flops | bytes accessed | tf_op | source)
XLA Modules:
  0.0 313.5 jit_solution(18282270828736118344)
XLA Ops:
  7.2 0.0 copy-start
  7.2 0.0 all-gather.4.cloned.1.call-start
  7.2 0.8 fusion.32
  8.1 0.4 convert_reduce_fusion
  8.5 0.3 convolution_convert_fusion.2
  8.7 1.8 convolution_convert_fusion.1
  10.5 0.0 all-gather.4.cloned.1.call-update
  10.6 0.0 all-gather.6.cloned.1.call-start
  10.6 0.0 copy-done
  10.6 4.5 %gather_fusion = s32[768]{0:T(1024)S(1)} fusion(s32[6144]{0:T(1024)S(1)} %copy-done, s32[1024]{0:T(1024)S(1)} %get-tuple-element.25), kind=kCustom, calls=%fused_computation | custom fusion | bytes 9216 | tf_op jit(solution)/shard_map/gather | solution.py:10
  15.1 0.0 copy-start.2
  15.1 4.5 %gather_fusion.1 = s32[768]{0:T(1024)S(1)} fusion(s32[6144]{0:T(1024)S(1)} %copy-done, s32[1024]{0:T(1024)S(1)} %get-tuple-element.24), kind=kCustom, calls=%fused_computation.1 | custom fusion | bytes 9216 | tf_op jit(solution)/shard_map/gather | solution.py:11
  19.6 0.3 convert_reduce_fusion.2
  20.0 0.8 fusion.14
  20.8 65.7 %all-gather.4.cloned.1.call-done = bf16[768,768]{1,0:T(8,128)(2,1)} async-done(((bf16[24,768]{1,0:T(8,128)(2,1)}), bf16[768,768]{1,0:T(8,128)(2,1)}) %all-gather.4.cloned.1.call-update) | async-done | bytes 1179664 | tf_op jit(solution)/shard_map/all_gather | solution.py:86
  86.5 0.0 copy-done.2
  86.5 2.4 fusion.13
  88.9 0.0 all-gather.6.cloned.1.call-update
  88.9 0.0 copy-start.1
  88.9 0.2 all-gather.8.cloned.1.call-start
  89.1 4.3 %convolution_convert_fusion = bf16[24,14232]{1,0:T(8,128)(2,1)} fusion(bf16[24,192]{1,0:T(8,128)(2,1)S(1)} %convolution_convert_fusion.2, bf16[192,14232]{1,0:T(8,128)(2,1)} %param.5), kind=kOutput, calls=%fused_computation.7 | convolution fusion | flops 131503680 | bytes 6157440 | tf_op jit(solution)/shard_map/dot_general | solution.py:72
  93.4 0.0 all-gather.8.cloned.1.call-update
  93.4 0.4 fusion.6
  93.8 0.9 convert_reduce_fusion.1
  94.7 25.4 %all-gather.6.cloned.1.call-done = bf16[192,6144]{1,0:T(8,128)(2,1)} async-done(((bf16[192,768]{1,0:T(8,128)(2,1)}), bf16[192,6144]{1,0:T(8,128)(2,1)}) %all-gather.6.cloned.1.call-update) | async-done | bytes 2359312 | tf_op jit(solution)/shard_map/all_gather | solution.py:107
  120.1 0.0 copy-done.1
  120.1 6.4 %fusion.12 = bf16[192,768]{1,0:T(8,128)(2,1)} fusion(bf16[192,6144]{1,0:T(8,128)(2,1)} %all-gather.6.cloned.1.call-done, s32[768]{0:T(1024)S(1)} %fusion.6, bf16[192,768]{1,0:T(8,128)(2,1)S(1)} %copy-done.1, f32[768]{0:T(1024)S(1)} %get-tuple-element.3, f32[768]{0:T(1024)S(1)} %subtract_add_fusion), kind=kOutput, calls=%fused_computation.26 | convolution fusion | flops 1817395200 | bytes 2958336 | tf_op jit(solution)/shard_map/dot_general | solution.py:112
  126.5 162.6 %all-gather.8.cloned.1.call-done = bf16[768,14232]{1,0:T(8,128)(2,1)} async-done(((bf16[24,14232]{1,0:T(8,128)(2,1)}), bf16[768,14232]{1,0:T(8,128)(2,1)}) %all-gather.8.cloned.1.call-update) | async-done | bytes 21860368 | tf_op jit(solution)/shard_map/all_gather | solution.py:91
  289.1 17.9 %fusion.2 = bf16[192,14232]{1,0:T(8,128)(2,1)} fusion(bf16[192,768]{1,0:T(8,128)(2,1)S(1)} %fusion.14, bf16[768,14232]{1,0:T(8,128)(2,1)} %all-gather.8.cloned.1.call-done, bf16[192,14232]{1,0:T(8,128)(2,1)} %param.5, f32[192]{0:T(256)S(1)} %get-tuple-element.12, f32[192]{0:T(256)S(1)} %subtract_add_fusion.1), kind=kOutput, calls=%fused_computation.6 | convolution fusion | flops 4210850304 | bytes 33086976 | tf_op jit(solution)/shard_map/dot_general | solution.py:89
  (10 shorter events, 0.1 us)
Async XLA Ops:
  7.2 3.5 %copy-start = (s32[6144]{0:T(1024)S(1)}, s32[6144]{0:T(1024)}, u32[]{:S(2)}) copy-start(s32[6144]{0:T(1024)} %param.7) | copy-start | bytes 73732
  7.2 79.3 %all-gather.4.cloned.1.call-start = ((), (), s32[]{:S(2)}) async-start(), calls=%async_computation | async-start | bytes 1216512 | tf_op jit(solution)/shard_map/all_gather | solution.py:86
  10.6 109.6 %all-gather.6.cloned.1.call-start = ((), (), s32[]{:S(2)}) async-start(), calls=%async_computation.1 | async-start | bytes 2654208 | tf_op jit(solution)/shard_map/all_gather | solution.py:107
  15.1 71.4 %copy-start.2 = (bf16[192,768]{1,0:T(8,128)(2,1)S(1)}, bf16[192,768]{1,0:T(8,128)(2,1)}, u32[]{:S(2)}) copy-start(bf16[192,768]{1,0:T(8,128)(2,1)} %param.4) | copy-start | bytes 884740
  88.9 31.2 %copy-start.1 = (bf16[192,768]{1,0:T(8,128)(2,1)S(1)}, bf16[192,768]{1,0:T(8,128)(2,1)}, u32[]{:S(2)}) copy-start(bf16[192,768]{1,0:T(8,128)(2,1)} %fusion.13) | copy-start | bytes 884740
  88.9 200.2 %all-gather.8.cloned.1.call-start = ((), (), s32[]{:S(2)}) async-start(), calls=%async_computation.2 | async-start | bytes 22708224 | tf_op jit(solution)/shard_map/all_gather | solution.py:91
Sparse Core Ops, SparseCore 0:
  11.1 75.2 all-gather.3
  89.0 31.0 all-gather.5
  123.3 165.8 all-gather.7
where the time goes:
time: 314 us
  waiting for transfers between devices  254 us (81%)
  matrix products  33.7 us (11%)
  between operations  13.9 us (4%)
  local copies, waits for them, and re-layouts  8.95 us (3%)
    all_gather x1, waiting for transfers between devices, shards(): lax.all_gather(send_rest, 'row', axis=0, tiled=True)  163 us
    all_gather x1, waiting for transfers between devices, shards(): lax.all_gather(send_window, 'row', axis=0, tiled=True)  65.7 us
    all_gather x1, waiting for transfers between devices, shards(): piece = lax.all_gather(mixed_window, 'col', axis=1, tiled=True)  25.4 us
    dot_general x1, matrix products, shards(): jnp.dot(placement, lax.all_gather(send_rest, 'row', axis=0, tiled=True),...  17.9 us
    dot_general x1, matrix products, shards(): gathered = jnp.dot(piece, picker, preferred_element_type=jnp.float32)  6.39 us
  transfers between devices with their start and end apart: 3, of which 3 were waited for; matrix products, arithmetic and copies ran while one was open for 7% of the time, Pallas kernels for 0%

commit v1 on v0

--- a/solution.py
+++ b/solution.py
@@ -83,7 +83,9 @@
     )
     placed_window = jnp.dot(
         placement,
-        lax.all_gather(send_window, "row", axis=0, tiled=True),
+        jnp.concatenate(
+            lax.all_to_all(jnp.stack([send_window] * lax.axis_size("row")), "row", 0, 0), axis=0
+        ),
         preferred_element_type=jnp.float32,
     )
     placed_rest = jnp.dot(

time: 314 us -> 275 us (0.88)
  waiting for transfers between devices: 254 us -> 204 us
  starting transfers between devices: 0.3 us -> 12.3 us
    all_gather x1 -> x0, waiting for transfers between devices: 65.7 us -> none  [shards(): lax.all_gather(send_window, 'row', axis=0, tiled=True)]
    all_to_all x0 -> x1, waiting for transfers between devices: none -> 17.3 us  [shards(): lax.all_to_all(jnp.stack([send_window] * lax.axis_size('row')), 'row', 0, 0)]
    all_to_all x0 -> x1, starting transfers between devices: none -> 12 us  [shards(): lax.all_to_all(jnp.stack([send_window] * lax.axis_size('row')), 'row', 0, 0)]
  transfers between devices with their start and end apart: 3 -> 3, of which waited for: 3 -> 3; matrix products, arithmetic and copies ran while one was open for 7% -> 8% of each run, Pallas kernels for 0% -> 0%
where the time goes in v1:
time: 275 us
  waiting for transfers between devices  204 us (74%)
  matrix products  31.8 us (12%)
  between operations  14.2 us (5%)
  starting transfers between devices  12.3 us (4%)
  local copies, waits for them, and re-layouts  10 us (4%)
  other arithmetic  2.91 us (1%)
    all_gather x1, waiting for transfers between devices, shards(): lax.all_gather(send_rest, 'row', axis=0, tiled=True)  163 us
    all_gather x1, waiting for transfers between devices, shards(): piece = lax.all_gather(mixed_window, 'col', axis=1, tiled=True)  23.6 us
    dot_general x1, matrix products, shards(): jnp.dot(placement, lax.all_gather(send_rest, 'row', axis=0, tiled=True),...  17.9 us
    all_to_all x1, waiting for transfers between devices, shards(): lax.all_to_all(jnp.stack([send_window] * lax.axis_size('row')), 'row', 0, 0)  17.3 us
    all_to_all x1, starting transfers between devices, shards(): lax.all_to_all(jnp.stack([send_window] * lax.axis_size('row')), 'row', 0, 0)  12 us
    dot_general x1, matrix products, shards(): gathered = jnp.dot(piece, picker, preferred_element_type=jnp.float32)  6.39 us
  transfers between devices with their start and end apart: 3, of which 3 were waited for; matrix products, arithmetic and copies ran while one was open for 8% of the time, Pallas kernels for 0%

profile of v1, /device:TPU:1, one launch (start us, length us, event | category | flops | bytes accessed | tf_op | source)
XLA Modules:
  0.0 274.8 jit_solution(7704345066781727186)
XLA Ops:
  7.2 0.0 copy-start
  7.2 0.8 fusion.32
  8.0 0.4 convert_reduce_fusion
  8.4 0.3 convolution_convert_fusion.2
  8.7 1.2 convolution_convert_fusion.1
  9.9 1.1 stack.2
  11.0 12.0 %all-to-all-start = ((bf16[32,24,768]{2,1,0:T(8,128)(2,1)}), bf16[32,24,768]{2,1,0:T(8,128)(2,1)S(1)}, u32[]{:S(2)}, u32[]{:S(2)}) async-start(bf16[32,24,768]{2,1,0:T(8,128)(2,1)} %stack.2), calls=%async_computation | async-start | bytes 2359296 | tf_op jit(solution)/shard_map/all_to_all | solution.py:87
  23.0 0.0 all-gather.3.cloned.1.call-start
  23.1 0.0 copy-done
  23.1 4.5 %gather_fusion = s32[768]{0:T(1024)S(1)} fusion(s32[6144]{0:T(1024)S(1)} %copy-done, s32[1024]{0:T(1024)S(1)} %get-tuple-element.25), kind=kCustom, calls=%fused_computation | custom fusion | bytes 9216 | tf_op jit(solution)/shard_map/gather | solution.py:10
  27.5 0.0 copy-start.2
  27.5 4.5 %gather_fusion.1 = s32[768]{0:T(1024)S(1)} fusion(s32[6144]{0:T(1024)S(1)} %copy-done, s32[1024]{0:T(1024)S(1)} %get-tuple-element.24), kind=kCustom, calls=%fused_computation.1 | custom fusion | bytes 9216 | tf_op jit(solution)/shard_map/gather | solution.py:11
  32.1 0.3 convert_reduce_fusion.2
  32.4 0.8 fusion.14
  33.2 17.3 %all-to-all-done = bf16[32,24,768]{2,1,0:T(8,128)(2,1)S(1)} async-done(((bf16[32,24,768]{2,1,0:T(8,128)(2,1)}), bf16[32,24,768]{2,1,0:T(8,128)(2,1)S(1)}, u32[]{:S(2)}, u32[]{:S(2)}) %all-to-all-start) | async-done | bytes 1179680 | tf_op jit(solution)/shard_map/all_to_all | solution.py:87
  50.5 0.0 copy-done.2
  50.5 1.1 fusion.13
  51.7 0.0 all-gather.3.cloned.1.call-update
  51.7 0.0 copy-start.1
  51.7 0.2 all-gather.5.cloned.1.call-start
  51.9 4.3 %convolution_convert_fusion = bf16[24,14232]{1,0:T(8,128)(2,1)} fusion(bf16[24,192]{1,0:T(8,128)(2,1)S(1)} %convolution_convert_fusion.2, bf16[192,14232]{1,0:T(8,128)(2,1)} %param.5), kind=kOutput, calls=%fused_computation.7 | convolution fusion | flops 131503680 | bytes 6157440 | tf_op jit(solution)/shard_map/dot_general | solution.py:72
  56.2 0.0 all-gather.5.cloned.1.call-update
  56.2 0.4 fusion.6
  56.6 0.9 convert_reduce_fusion.1
  57.5 23.6 %all-gather.3.cloned.1.call-done = bf16[192,6144]{1,0:T(8,128)(2,1)} async-done(((bf16[192,768]{1,0:T(8,128)(2,1)}), bf16[192,6144]{1,0:T(8,128)(2,1)}) %all-gather.3.cloned.1.call-update) | async-done | bytes 2359312 | tf_op jit(solution)/shard_map/all_gather | solution.py:109
  81.1 0.0 copy-done.1
  81.1 6.4 %fusion.12 = bf16[192,768]{1,0:T(8,128)(2,1)} fusion(bf16[192,6144]{1,0:T(8,128)(2,1)} %all-gather.3.cloned.1.call-done, s32[768]{0:T(1024)S(1)} %fusion.6, bf16[192,768]{1,0:T(8,128)(2,1)S(1)} %copy-done.1, f32[768]{0:T(1024)S(1)} %get-tuple-element.3, f32[768]{0:T(1024)S(1)} %subtract_add_fusion), kind=kOutput, calls=%fused_computation.26 | convolution fusion | flops 1817395200 | bytes 2958336 | tf_op jit(solution)/shard_map/dot_general | solution.py:114
  87.5 162.6 %all-gather.5.cloned.1.call-done = bf16[768,14232]{1,0:T(8,128)(2,1)} async-done(((bf16[24,14232]{1,0:T(8,128)(2,1)}), bf16[768,14232]{1,0:T(8,128)(2,1)}) %all-gather.5.cloned.1.call-update) | async-done | bytes 21860368 | tf_op jit(solution)/shard_map/all_gather | solution.py:93
  250.1 17.9 %fusion.2 = bf16[192,14232]{1,0:T(8,128)(2,1)} fusion(bf16[192,768]{1,0:T(8,128)(2,1)S(1)} %fusion.14, bf16[768,14232]{1,0:T(8,128)(2,1)} %all-gather.5.cloned.1.call-done, bf16[192,14232]{1,0:T(8,128)(2,1)} %param.5, f32[192]{0:T(256)S(1)} %get-tuple-element.12, f32[192]{0:T(256)S(1)} %subtract_add_fusion.1), kind=kOutput, calls=%fused_computation.6 | convolution fusion | flops 4210850304 | bytes 33086976 | tf_op jit(solution)/shard_map/dot_general | solution.py:91
  (10 shorter events, 0.1 us)
Async XLA Ops:
  7.2 15.9 %copy-start = (s32[6144]{0:T(1024)S(1)}, s32[6144]{0:T(1024)}, u32[]{:S(2)}) copy-start(s32[6144]{0:T(1024)} %param.7) | copy-start | bytes 73732
  11.0 39.6 %all-to-all-start = ((bf16[32,24,768]{2,1,0:T(8,128)(2,1)}), bf16[32,24,768]{2,1,0:T(8,128)(2,1)S(1)}, u32[]{:S(2)}, u32[]{:S(2)}) async-start(bf16[32,24,768]{2,1,0:T(8,128)(2,1)} %stack.2), calls=%async_computation | async-start | bytes 2359296 | tf_op jit(solution)/shard_map/all_to_all | solution.py:87
  23.0 58.1 %all-gather.3.cloned.1.call-start = ((), (), s32[]{:S(2)}) async-start(), calls=%async_computation.1 | async-start | bytes 2654208 | tf_op jit(solution)/shard_map/all_gather | solution.py:109
  27.5 23.0 %copy-start.2 = (bf16[192,768]{1,0:T(8,128)(2,1)S(1)}, bf16[192,768]{1,0:T(8,128)(2,1)}, u32[]{:S(2)}) copy-start(bf16[192,768]{1,0:T(8,128)(2,1)} %param.4) | copy-start | bytes 884740
  51.7 29.4 %copy-start.1 = (bf16[192,768]{1,0:T(8,128)(2,1)S(1)}, bf16[192,768]{1,0:T(8,128)(2,1)}, u32[]{:S(2)}) copy-start(bf16[192,768]{1,0:T(8,128)(2,1)} %fusion.13) | copy-start | bytes 884740
  51.7 198.4 %all-gather.5.cloned.1.call-start = ((), (), s32[]{:S(2)}) async-start(), calls=%async_computation.2 | async-start | bytes 22708224 | tf_op jit(solution)/shard_map/all_gather | solution.py:93
Sparse Core Ops, SparseCore 0:
  51.8 29.2 all-gather.2
  84.2 165.8 all-gather.4
